TPU v7x, 32 devices: a whole 2x2x4 slice. The times are simulated.
32 devices in a mesh: dp: 8 (over y, x, core), mp: 4 (over z).
Axes of the slice: x: 2, y: 2, z: 4, core: 2. Of those that a mesh axis runs over, the one named last changes fastest.
Arguments:
- tokens: bfloat16 [8192, 2048], P('dp'), may hold values from -6 to 6
- doc_lengths: int32 [8, 8], P('dp'), may hold values from 1 to 512, 1024 in all within a row
- slot_live: int32 [36], P('mp'), may hold values from 0 to 1, as said below
- attn_gain: bfloat16 [2048], replicated, may hold values from 0.5 to 1.5
- w_query: bfloat16 [2048, 1536], P(None, 'mp'), may hold values from -0.125 to 0.125
- w_keyval: bfloat16 [2048, 768], replicated, may hold values from -0.125 to 0.125
- q_gain: bfloat16 [64], replicated, may hold values from 0.099609375 to 1.8984375
- k_gain: bfloat16 [64], replicated, may hold values from 0.099609375 to 1.8984375
- w_out: bfloat16 [1536, 2048], P('mp'), may hold values from -0.625 to 0.625
- ffn_gain: bfloat16 [2048], replicated, may hold values from 0.5 to 1.5
- w_gate: bfloat16 [2048, 4608], P(None, 'mp'), may hold values from -0.125 to 0.125
- w_up: bfloat16 [2048, 4608], P(None, 'mp'), may hold values from -0.125 to 0.125
- w_down: bfloat16 [4608, 2048], P('mp'), may hold values from -0.09375 to 0.09375
- out_grad: bfloat16 [8192, 2048], P('dp'), may hold values from -6 to 6
Outputs:
- block_out: bfloat16 [8192, 2048], P(('dp', 'mp'))
- grad_tokens: float32 [8192, 2048], P(('dp', 'mp'))
- grad_attn_gain: float32 [2048], replicated
- grad_query: float32 [2048, 1536], P('dp', 'mp')
- grad_keyval: float32 [2048, 768], P(('dp', 'mp'))
- grad_q_gain: float32 [64], replicated
- grad_k_gain: float32 [64], replicated
- grad_out_proj: float32 [1536, 2048], P('mp', 'dp')
- grad_ffn_gain: float32 [2048], replicated
- grad_gate: float32 [2048, 4608], P('dp', 'mp')
- grad_up: float32 [2048, 4608], P('dp', 'mp')
- grad_down: float32 [4608, 2048], P('mp', 'dp')
Inputs may be any that keep to these rules, and one draw needn't show every extreme that they name: `doc_lengths`: each row's 8 lengths sum to 1024, and one of them is 512. `slot_live`: the 9 slots of each index of mp hold 34 // 4 or 34 // 4 + 1 live ones, 34 live in all; which slots and which indices hold more varies.
All inputs are finite; a program needn't handle non-finite values.
Results may differ from a plain program's by a relative error of at most 0.018.
Values may be sent and summed in bfloat16 or wider, within the bound.
A program may use at most 192 MiB of HBM per device.

v0:
```python
import math
import jax
import jax.numpy as jnp
from jax import lax
from jax.sharding import PartitionSpec as P

EPSILON = 1e-06
MASKED = -1000000000.0
ROPE_BASE = 10000.0
HIGHEST_PREC = lax.Precision.HIGHEST
CONTRACT_LAST = (((1,), (1,)), ((), ()))
CONTRACT_FIRST = (((0,), (0,)), ((), ()))


def normalize(raw_in):
    return raw_in * lax.rsqrt(jnp.mean(raw_in * raw_in, axis=-1, keepdims=True) + EPSILON)


def norm_back(grad_normed, raw_in, gain_vec):
    factor = lax.rsqrt(jnp.mean(raw_in * raw_in, axis=-1, keepdims=True) + EPSILON)
    unit_rows = raw_in * factor
    scaled = grad_normed * gain_vec
    grad_raw = factor * (scaled - unit_rows * jnp.mean(scaled * unit_rows, axis=-1, keepdims=True))
    return (grad_raw, jnp.sum(grad_normed * unit_rows, axis=tuple(range(raw_in.ndim - 1))))


def rotate(values, cosine_tab, sine_tab, sign):
    half_size = values.shape[-1] // 2
    first_half = values[..., :half_size]
    second_half = values[..., half_size:]
    return jnp.concatenate(
        [
            first_half * cosine_tab - sign * second_half * sine_tab,
            second_half * cosine_tab + sign * first_half * sine_tab,
        ],
        axis=-1,
    )


def doc_layout(lengths, row_count):
    doc_ends = jnp.cumsum(lengths)
    token_index = jnp.arange(row_count, dtype=jnp.int32)
    past_end = (token_index[:, None] >= doc_ends[None, :]).astype(jnp.int32)
    doc_id = jnp.sum(past_end, axis=1)
    doc_pos = token_index - jnp.sum(past_end * lengths[None, :], axis=1)
    return (doc_id, doc_pos, token_index)


def rope_table(doc_pos, head_size):
    rope_freq = jnp.exp(
        jnp.arange(head_size // 2, dtype=jnp.float32) * (-2.0 * math.log(ROPE_BASE) / head_size)
    )
    rope_angle = doc_pos.astype(jnp.float32)[:, None] * rope_freq[None, :]
    return (jnp.cos(rope_angle)[:, None, :], jnp.sin(rope_angle)[:, None, :])


def shards(
    tokens,
    doc_lengths,
    slot_live,
    attn_gain,
    w_query,
    w_keyval,
    q_gain,
    k_gain,
    w_out,
    ffn_gain,
    w_gate,
    w_up,
    w_down,
    out_grad,
):
    row_count, model_width = tokens.shape
    head_size = q_gain.shape[0]
    heads_dev = w_query.shape[1] // head_size
    heads_all = heads_dev * lax.axis_size("mp")
    kv_heads = w_keyval.shape[1] // (2 * head_size)
    group_size = heads_all // kv_heads
    kv_window = min(kv_heads, (heads_dev + group_size - 2) // group_size + 1)
    tile_cols = w_gate.shape[1] // slot_live.shape[0]
    shard_rows = row_count // lax.axis_size("mp")
    block_rows = min(512, row_count)
    score_scale = head_size ** (-0.5)
    head_span = heads_dev * head_size
    mp_index = lax.axis_index("mp")
    row_first = mp_index * shard_rows
    q_first = mp_index * heads_dev
    kv_first = jnp.minimum(q_first // group_size, kv_heads - kv_window)
    kv_owner = (q_first + jnp.arange(heads_dev, dtype=jnp.int32)) // group_size - kv_first
    head_pick = (kv_owner[:, None] == jnp.arange(kv_window, dtype=jnp.int32)[None, :]).astype(
        jnp.float32
    )
    key_cols = lax.dynamic_slice_in_dim(w_keyval, kv_first * head_size, kv_window * head_size, 1)
    value_cols = lax.dynamic_slice_in_dim(
        w_keyval, (kv_heads + kv_first) * head_size, kv_window * head_size, 1
    )

    def spread(window_cols):
        return (
            jnp.einsum(
                "dwe,hw->dhe",
                window_cols.reshape(model_width, kv_window, head_size),
                head_pick.astype(jnp.bfloat16),
                preferred_element_type=jnp.float32,
            )
            .astype(jnp.bfloat16)
            .reshape(model_width, head_span)
        )

    def fold_heads(per_head):
        return jnp.einsum(
            "dhe,hw->dwe",
            per_head.reshape(model_width, heads_dev, head_size),
            head_pick,
            precision=HIGHEST_PREC,
        ).reshape(model_width, kv_window * head_size)

    doc_id, doc_pos, token_index = doc_layout(doc_lengths[0], row_count)
    cosine_tab, sine_tab = rope_table(doc_pos, head_size)
    x_float = tokens.astype(jnp.float32)
    x_rows = lax.dynamic_slice_in_dim(x_float, row_first, shard_rows, 0)
    gain_one = attn_gain.astype(jnp.float32)
    gain_two = ffn_gain.astype(jnp.float32)
    q_gain_f = q_gain.astype(jnp.float32)
    k_gain_f = k_gain.astype(jnp.float32)
    xn_one = (normalize(x_float) * gain_one).astype(jnp.bfloat16)
    q_raw = jnp.dot(xn_one, w_query, preferred_element_type=jnp.float32).reshape(
        row_count, heads_dev, head_size
    )
    kv_raw = jnp.dot(
        xn_one, jnp.concatenate([key_cols, value_cols], axis=1), preferred_element_type=jnp.float32
    ).reshape(row_count, 2, kv_window, head_size)
    k_raw = jnp.einsum("twe,hw->the", kv_raw[:, 0], head_pick, precision=HIGHEST_PREC)
    v_raw = jnp.einsum("twe,hw->the", kv_raw[:, 1], head_pick, precision=HIGHEST_PREC)
    q_rot = rotate(normalize(q_raw) * q_gain_f, cosine_tab, sine_tab, 1.0).astype(jnp.bfloat16)
    k_rot = rotate(normalize(k_raw) * k_gain_f, cosine_tab, sine_tab, 1.0).astype(jnp.bfloat16)
    v_low = v_raw.astype(jnp.bfloat16)

    def block_scores(row_start, key_stop):
        scores = (
            jnp.einsum(
                "qhe,khe->hqk",
                q_rot[row_start : row_start + block_rows],
                k_rot[:key_stop],
                preferred_element_type=jnp.float32,
            )
            * score_scale
        )
        allowed = (doc_id[row_start : row_start + block_rows, None] == doc_id[None, :key_stop]) & (
            token_index[None, :key_stop] <= token_index[row_start : row_start + block_rows, None]
        )
        return jnp.where(allowed[None], scores, MASKED)

    block_outs = []
    block_lse = []
    for row_start in range(0, row_count, block_rows):
        key_stop = row_start + block_rows
        scores = block_scores(row_start, key_stop)
        row_max = jnp.max(scores, axis=-1, keepdims=True)
        shifted = jnp.exp(scores - row_max)
        row_total = jnp.sum(shifted, axis=-1, keepdims=True)
        attn_probs = (shifted / row_total).astype(jnp.bfloat16)
        block_outs.append(
            jnp.einsum(
                "hqk,khe->qhe", attn_probs, v_low[:key_stop], preferred_element_type=jnp.float32
            )
        )
        block_lse.append(row_max + jnp.log(row_total))
    attended = (
        jnp.concatenate(block_outs, axis=0).reshape(row_count, head_span).astype(jnp.bfloat16)
    )
    attn_part = jnp.dot(attended, w_out, preferred_element_type=jnp.float32)
    hidden_full = x_float + lax.psum(attn_part, "mp")
    hidden_rows = lax.dynamic_slice_in_dim(hidden_full, row_first, shard_rows, 0)
    xn_two = (normalize(hidden_full) * gain_two).astype(jnp.bfloat16)
    live_cols = jnp.repeat(slot_live.astype(jnp.float32), tile_cols)
    gate_act = jnp.dot(xn_two, w_gate, preferred_element_type=jnp.float32)
    up_act = jnp.dot(xn_two, w_up, preferred_element_type=jnp.float32)
    gate_sigmoid = jax.nn.sigmoid(gate_act)
    gate_silu = gate_act * gate_sigmoid
    ffn_hidden = (gate_silu * up_act * live_cols).astype(jnp.bfloat16)
    ffn_part = jnp.dot(ffn_hidden, w_down, preferred_element_type=jnp.float32)
    out_rows = hidden_rows + lax.psum_scatter(
        ffn_part.astype(jnp.bfloat16), "mp", scatter_dimension=0, tiled=True
    ).astype(jnp.float32)
    block_out = out_rows.astype(jnp.bfloat16)
    d_hidden = (
        lax.dot_general(out_grad, w_down, CONTRACT_LAST, preferred_element_type=jnp.float32)
        * live_cols
    )
    grad_down = lax.dot_general(
        ffn_hidden, out_grad, CONTRACT_FIRST, preferred_element_type=jnp.float32
    )
    d_gate = (d_hidden * up_act * gate_sigmoid * (1.0 + gate_act * (1.0 - gate_sigmoid))).astype(
        jnp.bfloat16
    )
    d_up = (d_hidden * gate_silu).astype(jnp.bfloat16)
    grad_gate = lax.dot_general(xn_two, d_gate, CONTRACT_FIRST, preferred_element_type=jnp.float32)
    grad_up = lax.dot_general(xn_two, d_up, CONTRACT_FIRST, preferred_element_type=jnp.float32)
    dn_two_part = lax.dot_general(
        d_gate, w_gate, CONTRACT_LAST, preferred_element_type=jnp.float32
    ) + lax.dot_general(d_up, w_up, CONTRACT_LAST, preferred_element_type=jnp.float32)
    dn_two = lax.psum(dn_two_part, "mp")
    back_two, _ = norm_back(dn_two, hidden_full, gain_two)
    dh_full = out_grad.astype(jnp.float32) + back_two
    dh_rows = lax.dynamic_slice_in_dim(dh_full, row_first, shard_rows, 0)
    grad_gain_two = jnp.sum(
        lax.dynamic_slice_in_dim(dn_two, row_first, shard_rows, 0) * normalize(hidden_rows), axis=0
    )
    dh_low = dh_full.astype(jnp.bfloat16)
    grad_out_proj = lax.dot_general(
        attended, dh_low, CONTRACT_FIRST, preferred_element_type=jnp.float32
    )
    d_att = lax.dot_general(dh_low, w_out, CONTRACT_LAST, preferred_element_type=jnp.float32)
    d_att = d_att.astype(jnp.bfloat16).reshape(row_count, heads_dev, head_size)
    dq_blocks = []
    d_keys = jnp.zeros((row_count, heads_dev, head_size), jnp.float32)
    d_values = jnp.zeros((row_count, heads_dev, head_size), jnp.float32)
    for block_index, row_start in enumerate(range(0, row_count, block_rows)):
        key_stop = row_start + block_rows
        scores = block_scores(row_start, key_stop)
        attn_probs = jnp.exp(scores - block_lse[block_index])
        probs_low = attn_probs.astype(jnp.bfloat16)
        att_rows = d_att[row_start:key_stop]
        d_probs = jnp.einsum(
            "qhe,khe->hqk", att_rows, v_low[:key_stop], preferred_element_type=jnp.float32
        )
        d_scores = (
            attn_probs * (d_probs - jnp.sum(d_probs * attn_probs, axis=-1, keepdims=True))
        ).astype(jnp.bfloat16)
        dq_blocks.append(
            jnp.einsum(
                "hqk,khe->qhe", d_scores, k_rot[:key_stop], preferred_element_type=jnp.float32
            )
            * score_scale
        )
        d_keys = d_keys.at[:key_stop].add(
            jnp.einsum(
                "hqk,qhe->khe",
                d_scores,
                q_rot[row_start:key_stop],
                preferred_element_type=jnp.float32,
            )
            * score_scale
        )
        d_values = d_values.at[:key_stop].add(
            jnp.einsum("hqk,qhe->khe", probs_low, att_rows, preferred_element_type=jnp.float32)
        )
    d_queries = jnp.concatenate(dq_blocks, axis=0)
    dq_raw, grad_q_gain = norm_back(rotate(d_queries, cosine_tab, sine_tab, -1.0), q_raw, q_gain_f)
    dk_raw, grad_k_gain = norm_back(rotate(d_keys, cosine_tab, sine_tab, -1.0), k_raw, k_gain_f)
    d_proj = jnp.concatenate(
        [
            dq_raw.reshape(row_count, head_span),
            dk_raw.reshape(row_count, head_span),
            d_values.reshape(row_count, head_span),
        ],
        axis=1,
    ).astype(jnp.bfloat16)
    w_proj = jnp.concatenate([w_query, spread(key_cols), spread(value_cols)], axis=1)
    dn_one_part = lax.dot_general(d_proj, w_proj, CONTRACT_LAST, preferred_element_type=jnp.float32)
    grad_proj = lax.dot_general(xn_one, d_proj, CONTRACT_FIRST, preferred_element_type=jnp.float32)
    grad_query = grad_proj[:, :head_span]
    grad_keyval = jnp.zeros((model_width, 2 * kv_heads * head_size), jnp.float32)
    grad_keyval = lax.dynamic_update_slice_in_dim(
        grad_keyval, fold_heads(grad_proj[:, head_span : 2 * head_span]), kv_first * head_size, 1
    )
    grad_keyval = lax.dynamic_update_slice_in_dim(
        grad_keyval, fold_heads(grad_proj[:, 2 * head_span :]), (kv_heads + kv_first) * head_size, 1
    )
    dn_one_rows = lax.psum_scatter(
        dn_one_part.astype(jnp.bfloat16), "mp", scatter_dimension=0, tiled=True
    ).astype(jnp.float32)
    back_one, grad_gain_one = norm_back(dn_one_rows, x_rows, gain_one)
    grad_tokens = dh_rows + back_one
    grad_query, grad_out_proj, grad_gate, grad_up, grad_down = (
        lax.psum_scatter(
            grad_query.astype(jnp.bfloat16), "dp", scatter_dimension=0, tiled=True
        ).astype(jnp.float32),
        lax.psum_scatter(
            grad_out_proj.astype(jnp.bfloat16), "dp", scatter_dimension=1, tiled=True
        ).astype(jnp.float32),
        lax.psum_scatter(
            grad_gate.astype(jnp.bfloat16), "dp", scatter_dimension=0, tiled=True
        ).astype(jnp.float32),
        lax.psum_scatter(
            grad_up.astype(jnp.bfloat16), "dp", scatter_dimension=0, tiled=True
        ).astype(jnp.float32),
        lax.psum_scatter(
            grad_down.astype(jnp.bfloat16), "dp", scatter_dimension=1, tiled=True
        ).astype(jnp.float32),
    )
    grad_keyval = lax.psum_scatter(grad_keyval, ("dp", "mp"), scatter_dimension=0, tiled=True)
    grad_gain_one, grad_gain_two, grad_q_gain, grad_k_gain = lax.psum(
        (grad_gain_one, grad_gain_two, grad_q_gain, grad_k_gain), ("dp", "mp")
    )
    return (
        block_out,
        grad_tokens,
        grad_gain_one,
        grad_query,
        grad_keyval,
        grad_q_gain,
        grad_k_gain,
        grad_out_proj,
        grad_gain_two,
        grad_gate,
        grad_up,
        grad_down,
    )


def solution(mesh):
    return jax.shard_map(
        shards,
        mesh=mesh,
        in_specs=(
            P("dp", None),
            P("dp", None),
            P("mp"),
            P(),
            P(None, "mp"),
            P(),
            P(),
            P(),
            P("mp", None),
            P(),
            P(None, "mp"),
            P(None, "mp"),
            P("mp", None),
            P("dp", None),
        ),
        out_specs=(
            P(("dp", "mp"), None),
            P(("dp", "mp"), None),
            P(),
            P("dp", "mp"),
            P(("dp", "mp"), None),
            P(),
            P(),
            P("mp", "dp"),
            P(),
            P("dp", "mp"),
            P("dp", "mp"),
            P("mp", "dp"),
        ),
        check_vma=False,
    )
```

profile of v0, /device:TPU:0, one launch (start us, length us, event | category | flops | bytes accessed | tf_op | source)
XLA Modules:
  0.0 1244.2 jit_solution(17080760547115743847)
XLA Ops:
  63.2 292.8 %all-reduce.6.cloned.1.call-done = f32[1024,2048]{1,0:T(8,128)} async-done(((f32[1024,2048]{1,0:T(8,128)}), f32[1024,2048]{1,0:T(8,128)}) %all-reduce.6.cloned.1.call-update) | async-done | bytes 8388624 | tf_op jit(solution)/shard_map/psum | solution.py:173
  364.9 11.4 fusion.111
  376.4 7.3 fusion.112
  383.7 12.7 %multiply_convert_fusion.4 = (bf16[1024,1152]{1,0:T(8,128)(2,1)S(1)}, bf16[1024,1152]{1,0:T(8,128)(2,1)}, bf16[1024,1152]{1,0:T(8,128)(2,1)}) fusion(f32[1024,1152]{1,0:T(8,128)} %fusion.111, f32[1024,1152]{1,0:T(8,128)} %fusion.112, f32[1152]{0:T(1024)S(1)} %broadcast_bitcast_fusion, bf16[1024,2048]{1,0:T(8,128)(2,1)S(1)} %copy-done.27, ...), kind=kOutput, calls=%fused_computation.36 | convolution fusion | flops 4851892224 | bytes 25432576 | tf_op jit(solution)/shard_map/dot_general | solution.py:188
  396.5 8.1 fusion.113
  404.6 8.5 convolution_add_fusion
  413.3 9.6 convolution_convert_fusion.2
  422.9 9.6 convolution_convert_fusion.1
  432.6 9.2 convolution_convert_fusion
  442.5 9.5 convolution_convert_fusion.3
  452.1 251.1 %all-reduce.8.cloned.1.call-done = f32[1024,2048]{1,0:T(8,128)} async-done(((f32[1024,2048]{1,0:T(8,128)}), f32[1024,2048]{1,0:T(8,128)}) %all-reduce.8.cloned.1.call-update) | async-done | bytes 8388624 | tf_op jit(solution)/shard_map/psum | solution.py:203
  703.2 6.9 multiply_reduce_fusion.1
  713.0 8.3 multiply_add_fusion
  748.9 6.9 multiply_convert_fusion
  792.5 7.4 fusion.19
  823.2 11.5 dynamic_update_slice.6
  834.7 11.0 dynamic_update_slice.7
  860.3 13.2 %reduce-scatter.23.cloned.1.call-done = bf16[1152,256]{1,0:T(8,128)(2,1)} async-done(((bf16[1152,2048]{1,0:T(8,128)(2,1)}), bf16[1152,256]{1,0:T(8,128)(2,1)}) %reduce-scatter.23.cloned.1.call-update) | async-done | bytes 589840 | tf_op jit(solution)/shard_map/reduce_scatter | solution.py:289
  875.8 76.7 %reduce-scatter.9.cloned.1.call-done = bf16[256,2048]{1,0:T(8,128)(2,1)} async-done(((bf16[1024,2048]{1,0:T(8,128)(2,1)}), bf16[256,2048]{1,0:T(8,128)(2,1)}) %reduce-scatter.9.cloned.1.call-update) | async-done | bytes 1048592 | tf_op jit(solution)/shard_map/reduce_scatter | solution.py:183
  956.6 38.2 %reduce-scatter.13.cloned.1.call-done = bf16[256,384]{0,1:T(8,128)(2,1)} async-done(((bf16[2048,384]{0,1:T(8,128)(2,1)}), bf16[256,384]{0,1:T(8,128)(2,1)}) %reduce-scatter.13.cloned.1.call-update) | async-done | bytes 196624 | tf_op jit(solution)/shard_map/reduce_scatter | solution.py:277
  996.5 39.9 %reduce-scatter.17.cloned.1.call-done = bf16[384,256]{1,0:T(8,128)(2,1)} async-done(((bf16[384,2048]{1,0:T(8,128)(2,1)}), bf16[384,256]{1,0:T(8,128)(2,1)}) %reduce-scatter.17.cloned.1.call-update) | async-done | bytes 196624 | tf_op jit(solution)/shard_map/reduce_scatter | solution.py:280
  1038.1 77.4 %reduce-scatter.11.cloned.1.call-done = bf16[256,2048]{1,0:T(8,128)(2,1)} async-done(((bf16[1024,2048]{1,0:T(8,128)(2,1)}), bf16[256,2048]{1,0:T(8,128)(2,1)}) %reduce-scatter.11.cloned.1.call-update) | async-done | bytes 1048592 | tf_op jit(solution)/shard_map/reduce_scatter | solution.py:271
  1118.2 41.1 %all-reduce.2 = (f32[2048]{0:T(1024)}, f32[64]{0:T(128)}, f32[64]{0:T(128)}, f32[2048]{0:T(1024)}) all-reduce(f32[2048]{0:T(1024)S(1)} %get-tuple-element.124, f32[64]{0:T(128)S(1)} %reduce_sum.217, f32[64]{0:T(128)S(1)} %get-tuple-element.126, f32[2048]{0:T(1024)S(1)} %get-tuple-element.141), channel_id=1, replica_groups=mesh['dp'=8,'mp'=4] {'dp','mp'}, use_global_device_ids=true, to_apply=%region_23.24 | all-reduce | flops 4224 | bytes 33792 | tf_op jit(solution)/shard_map/psum | solution.py:294
  1163.9 73.2 %reduce-scatter.15.cloned.1.call-done = f32[64,768]{1,0:T(8,128)} async-done(((f32[2048,768]{1,0:T(8,128)}), f32[64,768]{1,0:T(8,128)}) %reduce-scatter.15.cloned.1.call-update) | async-done | bytes 196624 | tf_op jit(solution)/shard_map/reduce_scatter | solution.py:293
  (289 shorter events, 187.0 us)
Async XLA Ops:
  7.2 49.6 %copy-start = (bf16[384,2048]{1,0:T(8,128)(2,1)S(1)}, bf16[384,2048]{1,0:T(8,128)(2,1)}, u32[]{:S(2)}) copy-start(bf16[384,2048]{1,0:T(8,128)(2,1)} %param.34) | copy-start | bytes 4718596
  7.2 348.8 %all-reduce.6.cloned.1.call-start = ((), (), s32[]{:S(2)}) async-start(), calls=%async_computation.8 | async-start | bytes 16777216 | tf_op jit(solution)/shard_map/psum | solution.py:173
  7.3 27.2 %copy-start.54 = (s32[6]{0:T(128)}, s32[6]{0:T(128)S(1)}, u32[]{:S(2)}) copy-start(s32[6]{0:T(128)S(1)} %fusion.88) | copy-start | bytes 76
  8.2 16.5 %copy-start.52 = (f32[2048]{0:T(1024)}, f32[2048]{0:T(1024)S(1)}, u32[]{:S(2)}) copy-start(f32[2048]{0:T(1024)S(1)} %convert_element_type.146) | copy-start | bytes 24580
  11.6 27.6 %copy-start.61 = (f32[64]{0:T(128)}, f32[64]{0:T(128)S(1)}, u32[]{:S(2)}) copy-start(f32[64]{0:T(128)S(1)} %convert_element_type.151) | copy-start | bytes 772
  15.1 24.2 %copy-start.10 = (f32[1024,384]{0,1:T(8,128)}, f32[1024,384]{0,1:T(8,128)S(1)}, u32[]{:S(2)}) copy-start(f32[1024,384]{0,1:T(8,128)S(1)} %fusion.103) | copy-start | bytes 4718596
  15.3 23.9 %copy-start.45 = (f32[1024,6]{0,1:T(8,128)}, f32[1024,6]{0,1:T(8,128)S(1)}, u32[]{:S(2)}) copy-start(f32[1024,6]{0,1:T(8,128)S(1)} %add_rsqrt_fusion.1) | copy-start | bytes 73732
  15.3 23.9 %copy-start.56 = (f32[64]{0:T(128)}, f32[64]{0:T(128)S(1)}, u32[]{:S(2)}) copy-start(f32[64]{0:T(128)S(1)} %convert_element_type.153) | copy-start | bytes 772
  37.4 16.6 %copy-start.36 = (bf16[512,6,64]{0,1,2:T(8,128)(2,1)}, bf16[512,6,64]{0,1,2:T(8,128)(2,1)S(1)}, u32[]{:S(2)}) copy-start(bf16[512,6,64]{0,1,2:T(8,128)(2,1)S(1)} %slice.197) | copy-start | bytes 1179652
  62.5 640.7 %all-reduce.8.cloned.1.call-start = ((), (), s32[]{:S(2)}) async-start(), calls=%async_computation.10 | async-start | bytes 16777216 | tf_op jit(solution)/shard_map/psum | solution.py:203
  361.7 14.6 %slice-start.7 = ((s8[4718592]{0:T(1024)(128)(4,1)}), s8[524288]{0:T(1024)(128)(4,1)S(1)}, s32[]{:S(2)}) async-start(s8[4718592]{0:T(1024)(128)(4,1)} %bitcast.161), calls=%async_computation.25 | async-start | bytes 1048576
  376.4 20.1 %slice-start.5 = ((s8[4718592]{0:T(1024)(128)(4,1)}), s8[4194304]{0:T(1024)(128)(4,1)S(1)}, s32[]{:S(2)}) async-start(s8[4718592]{0:T(1024)(128)(4,1)} %bitcast.159), calls=%async_computation.23 | async-start | bytes 8388608
  376.4 28.3 %slice-start.9 = ((s8[4718592]{0:T(1024)(128)(4,1)}), s8[4194304]{0:T(1024)(128)(4,1)S(1)}, s32[]{:S(2)}) async-start(s8[4718592]{0:T(1024)(128)(4,1)} %bitcast.163), calls=%async_computation.27 | async-start | bytes 8388608
  383.7 20.9 %slice-start.10 = ((s8[4718592]{0:T(1024)(128)(4,1)}), s8[524288]{0:T(1024)(128)(4,1)S(1)}, s32[]{:S(2)}) async-start(s8[4718592]{0:T(1024)(128)(4,1)} %bitcast.163), calls=%async_computation.28 | async-start | bytes 1048576
  413.2 442.8 %reduce-scatter.19.cloned.1.call-start = ((), (), s32[]{:S(2)}) async-start(), calls=%async_computation.15 | async-start | bytes 5308416 | tf_op jit(solution)/shard_map/reduce_scatter | solution.py:283
  422.9 435.3 %reduce-scatter.21.cloned.1.call-start = ((), (), s32[]{:S(2)}) async-start(), calls=%async_computation.16 | async-start | bytes 5308416 | tf_op jit(solution)/shard_map/reduce_scatter | solution.py:286
  432.5 441.0 %reduce-scatter.23.cloned.1.call-start = ((), (), s32[]{:S(2)}) async-start(), calls=%async_computation.17 | async-start | bytes 5308416 | tf_op jit(solution)/shard_map/reduce_scatter | solution.py:289
  441.8 510.8 %reduce-scatter.9.cloned.1.call-start = ((), (), s32[]{:S(2)}) async-start(), calls=%async_computation.9 | async-start | bytes 5242880 | tf_op jit(solution)/shard_map/reduce_scatter | solution.py:183
  442.5 284.9 %copy-start.50 = (f32[6,512]{1,0:T(8,128)}, f32[6,512]{1,0:T(8,128)S(1)}, u32[]{:S(2)}) copy-start(f32[6,512]{1,0:T(8,128)S(1)} %log_add_fusion.1) | copy-start | bytes 36868
  452.0 542.7 %reduce-scatter.13.cloned.1.call-start = ((), (), s32[]{:S(2)}) async-start(), calls=%async_computation.12 | async-start | bytes 1769472 | tf_op jit(solution)/shard_map/reduce_scatter | solution.py:277
  710.1 17.3 %slice-start.3 = ((s8[6291456]{0:T(1024)(128)(4,1)}), s8[4194304]{0:T(1024)(128)(4,1)S(1)}, s32[]{:S(2)}) async-start(s8[6291456]{0:T(1024)(128)(4,1)} %bitcast.132), calls=%async_computation.21 | async-start | bytes 8388608
  779.3 257.2 %reduce-scatter.17.cloned.1.call-start = ((), (), s32[]{:S(2)}) async-start(), calls=%async_computation.14 | async-start | bytes 1769472 | tf_op jit(solution)/shard_map/reduce_scatter | solution.py:280
  785.7 329.8 %reduce-scatter.11.cloned.1.call-start = ((), (), s32[]{:S(2)}) async-start(), calls=%async_computation.11 | async-start | bytes 5242880 | tf_op jit(solution)/shard_map/reduce_scatter | solution.py:271
  799.9 437.2 %reduce-scatter.15.cloned.1.call-start = ((), (), s32[]{:S(2)}) async-start(), calls=%async_computation.13 | async-start | bytes 6488064 | tf_op jit(solution)/shard_map/reduce_scatter | solution.py:293
  (66 other events, 325.0 us)
Sparse Core Ops, SparseCore 0:
  62.6 293.3 all-reduce.5
  413.3 289.8 all-reduce.7
  706.6 52.7 reduce-scatter.18
  762.7 53.7 reduce-scatter.20
  819.9 53.6 reduce-scatter.22
  875.7 76.7 reduce-scatter.8
  955.8 38.8 reduce-scatter.12
  998.0 38.3 reduce-scatter.16
  1038.7 76.7 reduce-scatter.10
  1121.6 115.4 reduce-scatter.14
where the time goes:
time: 1250 us; the launch traced here: 1240 us
  waiting for transfers between devices  863 us (69%)
  matrix products  172 us (14%)
  other arithmetic  80.4 us (6%)
  local copies, waits for them, and re-layouts  71.4 us (6%)
  blocking collectives  41.1 us (3%)
  between operations  15.7 us (1%)
    psum x1, waiting for transfers between devices, shards(): hidden_full = x_float + lax.psum(attn_part, 'mp')  293 us
    psum x1, waiting for transfers between devices, shards(): dn_two = lax.psum(dn_two_part, 'mp')  251 us
    reduce_scatter x1, waiting for transfers between devices, shards(): lax.psum_scatter(dn_one_part.astype(jnp.bfloat16), 'mp', scatter_dimensio...  77.4 us
    reduce_scatter x1, waiting for transfers between devices, shards(): lax.psum_scatter(ffn_part.astype(jnp.bfloat16), 'mp', scatter_dimension=0...  76.7 us
    reduce_scatter x1, waiting for transfers between devices, shards(): lax.psum_scatter(grad_keyval, ('dp', 'mp'), scatter_dimension=0, tiled=True)  73.2 us
    psum x1, blocking collectives, shards(): lax.psum((grad_gain_one, grad_gain_two, grad_q_gain, grad_k_gain), ('dp',...  41.1 us
    reduce_scatter x1, waiting for transfers between devices, shards(): lax.psum_scatter(grad_out_proj.astype(jnp.bfloat16), 'dp', scatter_dimens...  39.9 us
    reduce_scatter x1, waiting for transfers between devices, shards(): lax.psum_scatter(grad_query.astype(jnp.bfloat16), 'dp', scatter_dimension...  38.2 us
  transfers between devices with their start and end apart: 10, of which 8 were waited for; matrix products, arithmetic and copies ran while one was open for 16% of the time, Pallas kernels for 0%

commit v1 on v0

--- a/solution.py
+++ b/solution.py
@@ -70,6 +70,19 @@
     w_down,
     out_grad,
 ):
+
+    def _open_local_data(local_array, named_axis="mp"):
+        q_n = lax.psum(1, named_axis)
+        e_now, upper = (local_array, 0)
+        while 1 << upper < q_n:
+            seen = []
+            for k0 in range(q_n):
+                seen.append((k0, k0 ^ 1 << upper))
+            z1 = lax.ppermute(e_now, named_axis, seen)
+            e_now = e_now + z1
+            upper = upper + 1
+        return e_now
+
     row_count, model_width = tokens.shape
     head_size = q_gain.shape[0]
     heads_dev = w_query.shape[1] // head_size
@@ -200,7 +213,7 @@
     dn_two_part = lax.dot_general(
         d_gate, w_gate, CONTRACT_LAST, preferred_element_type=jnp.float32
     ) + lax.dot_general(d_up, w_up, CONTRACT_LAST, preferred_element_type=jnp.float32)
-    dn_two = lax.psum(dn_two_part, "mp")
+    dn_two = _open_local_data(dn_two_part)
     back_two, _ = norm_back(dn_two, hidden_full, gain_two)
     dh_full = out_grad.astype(jnp.float32) + back_two
     dh_rows = lax.dynamic_slice_in_dim(dh_full, row_first, shard_rows, 0)

time: 1250 us -> 1410 us (1.13)
  waiting for transfers between devices: 863 us -> 1020 us
  other arithmetic: 80.4 us -> 96.7 us
    ppermute x0 -> x2, waiting for transfers between devices: none -> 584 us  [_open_local_data(): z1 = lax.ppermute(e_now, named_axis, seen)]
    psum x1 -> x0, waiting for transfers between devices: 251 us -> none  [shards(): dn_two = lax.psum(dn_two_part, 'mp')]
    reduce_scatter x1, waiting for transfers between devices: 76.7 us -> 0.01 us  [shards(): lax.psum_scatter(ffn_part.astype(jnp.bfloat16), 'mp', scatter_dimension=0...]
    reduce_scatter x1, waiting for transfers between devices: 39.9 us -> 0.01 us  [shards(): lax.psum_scatter(grad_out_proj.astype(jnp.bfloat16), 'dp', scatter_dimens...]
    reduce_scatter x1, waiting for transfers between devices: 38.2 us -> 0.01 us  [shards(): lax.psum_scatter(grad_query.astype(jnp.bfloat16), 'dp', scatter_dimension...]
  transfers between devices with their start and end apart: 10 -> 11, of which waited for: 8 -> 5; matrix products, arithmetic and copies ran while one was open for 16% -> 16% of each run, Pallas kernels for 0% -> 0%
where the time goes in v1:
time: 1410 us
  waiting for transfers between devices  1020 us (72%)
  matrix products  166 us (12%)
  other arithmetic  96.7 us (7%)
  local copies, waits for them, and re-layouts  69.7 us (5%)
  blocking collectives  41.2 us (3%)
  between operations  15.4 us (1%)
    ppermute x2, waiting for transfers between devices, _open_local_data(): z1 = lax.ppermute(e_now, named_axis, seen)  584 us
    psum x1, waiting for transfers between devices, shards(): hidden_full = x_float + lax.psum(attn_part, 'mp')  293 us
    reduce_scatter x1, waiting for transfers between devices, shards(): lax.psum_scatter(grad_keyval, ('dp', 'mp'), scatter_dimension=0, tiled=True)  73.3 us
    reduce_scatter x1, waiting for transfers between devices, shards(): lax.psum_scatter(dn_one_part.astype(jnp.bfloat16), 'mp', scatter_dimensio...  68.3 us
    psum x1, blocking collectives, shards(): lax.psum((grad_gain_one, grad_gain_two, grad_q_gain, grad_k_gain), ('dp',...  41.2 us
  transfers between devices with their start and end apart: 11, of which 5 were waited for; matrix products, arithmetic and copies ran while one was open for 16% of the time, Pallas kernels for 0%

profile of v1, /device:TPU:0, one launch (start us, length us, event | category | flops | bytes accessed | tf_op | source)
XLA Modules:
  0.0 1409.6 jit_solution(16432284653603223637)
XLA Ops:
  62.9 292.8 %all-reduce.5.cloned.1.call-done = f32[1024,2048]{1,0:T(8,128)} async-done(((f32[1024,2048]{1,0:T(8,128)}), f32[1024,2048]{1,0:T(8,128)}) %all-reduce.5.cloned.1.call-update) | async-done | bytes 8388624 | tf_op jit(solution)/shard_map/psum | solution.py:186
  364.7 11.7 fusion.111
  376.4 7.3 fusion.112
  383.7 12.1 multiply_convert_fusion.4
  397.2 7.4 convolution_convert_fusion.2
  404.6 8.5 fusion.113
  413.2 10.9 convolution_add_fusion
  424.0 7.3 convolution_convert_fusion.1
  431.4 175.0 %collective-permute-done = f32[1024,2048]{1,0:T(8,128)} collective-permute-done((f32[1024,2048]{1,0:T(8,128)}, f32[1024,2048]{1,0:T(8,128)}, u32[]{:S(2)}, u32[]{:S(2)}) %collective-permute-start) | collective-permute-done | bytes 8388640 | tf_op jit(solution)/shard_map/ppermute | solution.py:81
  606.4 11.8 add.217
  619.6 8.5 convolution_convert_fusion
  628.9 9.7 convolution_convert_fusion.3
  638.7 409.1 %collective-permute-done.1 = f32[1024,2048]{1,0:T(8,128)} collective-permute-done((f32[1024,2048]{1,0:T(8,128)}, f32[1024,2048]{1,0:T(8,128)}, u32[]{:S(2)}, u32[]{:S(2)}) %collective-permute-start.1) | collective-permute-done | bytes 8388640 | tf_op jit(solution)/shard_map/ppermute | solution.py:81
  1047.8 12.7 multiply_reduce_fusion.1
  1060.5 7.1 multiply_add_fusion
  1092.4 6.7 multiply_convert_fusion
  1122.4 6.4 convolution_convert_fusion.6
  1135.5 7.4 fusion.19
  1166.2 11.2 dynamic_update_slice.6
  1177.4 11.0 dynamic_update_slice.7
  1188.4 6.6 convert_element_type.145
  1212.9 68.3 %reduce-scatter.11.cloned.1.call-done = bf16[256,2048]{1,0:T(8,128)(2,1)} async-done(((bf16[1024,2048]{1,0:T(8,128)(2,1)}), bf16[256,2048]{1,0:T(8,128)(2,1)}) %reduce-scatter.11.cloned.1.call-update) | async-done | bytes 1048592 | tf_op jit(solution)/shard_map/reduce_scatter | solution.py:284
  1283.8 41.2 %all-reduce.2 = (f32[2048]{0:T(1024)}, f32[64]{0:T(128)}, f32[64]{0:T(128)}, f32[2048]{0:T(1024)}) all-reduce(f32[2048]{0:T(1024)S(1)} %get-tuple-element.124, f32[64]{0:T(128)S(1)} %reduce_sum.217, f32[64]{0:T(128)S(1)} %get-tuple-element.126, f32[2048]{0:T(1024)S(1)} %get-tuple-element.143), channel_id=1, replica_groups=mesh['dp'=8,'mp'=4] {'dp','mp'}, use_global_device_ids=true, to_apply=%region_22.23 | all-reduce | flops 4224 | bytes 33792 | tf_op jit(solution)/shard_map/psum | solution.py:307
  1329.5 73.3 %reduce-scatter.15.cloned.1.call-done = f32[64,768]{1,0:T(8,128)} async-done(((f32[2048,768]{1,0:T(8,128)}), f32[64,768]{1,0:T(8,128)}) %reduce-scatter.15.cloned.1.call-update) | async-done | bytes 196624 | tf_op jit(solution)/shard_map/reduce_scatter | solution.py:306
  (289 shorter events, 170.4 us)
Async XLA Ops:
  7.2 49.3 %copy-start = (bf16[384,2048]{1,0:T(8,128)(2,1)S(1)}, bf16[384,2048]{1,0:T(8,128)(2,1)}, u32[]{:S(2)}) copy-start(bf16[384,2048]{1,0:T(8,128)(2,1)} %param.34) | copy-start | bytes 4718596
  7.2 348.5 %all-reduce.5.cloned.1.call-start = ((), (), s32[]{:S(2)}) async-start(), calls=%async_computation.8 | async-start | bytes 16777216 | tf_op jit(solution)/shard_map/psum | solution.py:186
  7.3 26.9 %copy-start.56 = (s32[6]{0:T(128)}, s32[6]{0:T(128)S(1)}, u32[]{:S(2)}) copy-start(s32[6]{0:T(128)S(1)} %fusion.88) | copy-start | bytes 76
  8.2 16.2 %copy-start.54 = (f32[2048]{0:T(1024)}, f32[2048]{0:T(1024)S(1)}, u32[]{:S(2)}) copy-start(f32[2048]{0:T(1024)S(1)} %convert_element_type.146) | copy-start | bytes 24580
  11.6 27.4 %copy-start.63 = (f32[64]{0:T(128)}, f32[64]{0:T(128)S(1)}, u32[]{:S(2)}) copy-start(f32[64]{0:T(128)S(1)} %convert_element_type.151) | copy-start | bytes 772
  15.1 23.9 %copy-start.10 = (f32[1024,384]{0,1:T(8,128)}, f32[1024,384]{0,1:T(8,128)S(1)}, u32[]{:S(2)}) copy-start(f32[1024,384]{0,1:T(8,128)S(1)} %fusion.103) | copy-start | bytes 4718596
  15.3 23.6 %copy-start.47 = (f32[1024,6]{0,1:T(8,128)}, f32[1024,6]{0,1:T(8,128)S(1)}, u32[]{:S(2)}) copy-start(f32[1024,6]{0,1:T(8,128)S(1)} %add_rsqrt_fusion.1) | copy-start | bytes 73732
  15.3 23.6 %copy-start.58 = (f32[64]{0:T(128)}, f32[64]{0:T(128)S(1)}, u32[]{:S(2)}) copy-start(f32[64]{0:T(128)S(1)} %convert_element_type.153) | copy-start | bytes 772
  37.1 16.6 %copy-start.38 = (bf16[512,6,64]{0,1,2:T(8,128)(2,1)}, bf16[512,6,64]{0,1,2:T(8,128)(2,1)S(1)}, u32[]{:S(2)}) copy-start(bf16[512,6,64]{0,1,2:T(8,128)(2,1)S(1)} %slice.197) | copy-start | bytes 1179652
  62.2 1136.5 %reduce-scatter.19.cloned.1.call-start = ((), (), s32[]{:S(2)}) async-start(), calls=%async_computation.14 | async-start | bytes 5308416 | tf_op jit(solution)/shard_map/reduce_scatter | solution.py:296
  361.4 14.9 %slice-start.5 = ((s8[4718592]{0:T(1024)(128)(4,1)}), s8[524288]{0:T(1024)(128)(4,1)S(1)}, s32[]{:S(2)}) async-start(s8[4718592]{0:T(1024)(128)(4,1)} %bitcast.159), calls=%async_computation.22 | async-start | bytes 1048576
  364.7 31.1 %copy-start.30 = (bf16[1024,2048]{1,0:T(8,128)(2,1)}, bf16[1024,2048]{1,0:T(8,128)(2,1)S(1)}, u32[]{:S(2)}) copy-start(bf16[1024,2048]{1,0:T(8,128)(2,1)S(1)} %multiply_convert_fusion.1) | copy-start | bytes 12582916
  404.6 796.3 %reduce-scatter.21.cloned.1.call-start = ((), (), s32[]{:S(2)}) async-start(), calls=%async_computation.15 | async-start | bytes 5308416 | tf_op jit(solution)/shard_map/reduce_scatter | solution.py:299
  424.0 182.4 %collective-permute-start = (f32[1024,2048]{1,0:T(8,128)}, f32[1024,2048]{1,0:T(8,128)}, u32[]{:S(2)}, u32[]{:S(2)}) collective-permute-start(f32[1024,2048]{1,0:T(8,128)} %convolution_add_fusion), channel_id=1, source_target_pairs={{0,1},{1,0},{2,3},{3,2},{4,5},{5,4},{6,7},{7,6},{8,9},{9,8},{10,11... | collective-permute-start | bytes 25165832 | tf_op jit(solution)/shard_map/ppermute | solution.py:81
  431.4 771.6 %reduce-scatter.23.cloned.1.call-start = ((), (), s32[]{:S(2)}) async-start(), calls=%async_computation.16 | async-start | bytes 5308416 | tf_op jit(solution)/shard_map/reduce_scatter | solution.py:302
  431.4 188.2 %copy-start.28 = (bf16[1024,2048]{1,0:T(8,128)(2,1)S(1)}, bf16[1024,2048]{1,0:T(8,128)(2,1)}, u32[]{:S(2)}) copy-start(bf16[1024,2048]{1,0:T(8,128)(2,1)} %param.39) | copy-start | bytes 12582916
  618.2 429.6 %collective-permute-start.1 = (f32[1024,2048]{1,0:T(8,128)}, f32[1024,2048]{1,0:T(8,128)}, u32[]{:S(2)}, u32[]{:S(2)}) collective-permute-start(f32[1024,2048]{1,0:T(8,128)} %add.217), channel_id=1, source_target_pairs={{0,2},{1,3},{2,0},{3,1},{4,6},{5,7},{6,4},{7,5},{8,10},{9,11},{10,... | collective-permute-start | bytes 25165832 | tf_op jit(solution)/shard_map/ppermute | solution.py:81
  628.2 577.1 %reduce-scatter.9.cloned.1.call-start = ((), (), s32[]{:S(2)}) async-start(), calls=%async_computation.9 | async-start | bytes 5242880 | tf_op jit(solution)/shard_map/reduce_scatter | solution.py:196
  628.9 442.0 %copy-start.52 = (f32[6,512]{1,0:T(8,128)}, f32[6,512]{1,0:T(8,128)S(1)}, u32[]{:S(2)}) copy-start(f32[6,512]{1,0:T(8,128)S(1)} %log_add_fusion.1) | copy-start | bytes 36868
  638.7 570.7 %reduce-scatter.13.cloned.1.call-start = ((), (), s32[]{:S(2)}) async-start(), calls=%async_computation.11 | async-start | bytes 1769472 | tf_op jit(solution)/shard_map/reduce_scatter | solution.py:290
  638.7 421.8 %copy-start.29 = (bf16[1024,2048]{1,0:T(8,128)(2,1)S(1)}, bf16[1024,2048]{1,0:T(8,128)(2,1)}, u32[]{:S(2)}) copy-start(bf16[1024,2048]{1,0:T(8,128)(2,1)} %param.39) | copy-start | bytes 12582916
  1122.3 88.8 %reduce-scatter.17.cloned.1.call-start = ((), (), s32[]{:S(2)}) async-start(), calls=%async_computation.13 | async-start | bytes 1769472 | tf_op jit(solution)/shard_map/reduce_scatter | solution.py:293
  1128.8 152.4 %reduce-scatter.11.cloned.1.call-start = ((), (), s32[]{:S(2)}) async-start(), calls=%async_computation.10 | async-start | bytes 5242880 | tf_op jit(solution)/shard_map/reduce_scatter | solution.py:284
  1142.9 260.0 %reduce-scatter.15.cloned.1.call-start = ((), (), s32[]{:S(2)}) async-start(), calls=%async_computation.12 | async-start | bytes 6488064 | tf_op jit(solution)/shard_map/reduce_scatter | solution.py:306
  (67 other events, 312.6 us)
Sparse Core Ops, SparseCore 0:
  62.3 293.3 all-reduce.4
  404.7 52.7 reduce-scatter.18
  461.0 53.7 reduce-scatter.20
  628.3 52.7 reduce-scatter.22
  683.2 204.9 reduce-scatter.8
  1122.5 37.9 reduce-scatter.12
  1163.7 38.2 reduce-scatter.16
  1204.3 76.7 reduce-scatter.10
  1287.4 115.4 reduce-scatter.14
